TPU v7x, 32 devices: a whole 2x2x4 slice. The times are simulated.
32 devices in a mesh: data: 4 (over z), stage: 8 (over y, x, core).
Axes of the slice: x: 2, y: 2, z: 4, core: 2. Of those that a mesh axis runs over, the one named last changes fastest.
Arguments:
- master_up: float32 [8, 512, 2048], P('stage')
- master_down: float32 [8, 2048, 512], P('stage')
- mom1_up: float32 [8, 512, 2048], P('stage')
- mom1_down: float32 [8, 2048, 512], P('stage')
- mom2_up: float32 [8, 512, 2048], P('stage')
- mom2_down: float32 [8, 2048, 512], P('stage')
- grad_up: float32 [4, 8, 512, 2048], P('data', 'stage')
- grad_down: float32 [4, 8, 2048, 512], P('data', 'stage')
- stage_acts: bfloat16 [8, 2048, 512], P('stage', 'data')
- loss_grad: bfloat16 [2048, 512], P('data')
- next_batch: bfloat16 [16, 2048, 512], P(None, 'data')
- learn_rate: float32 [], replicated
- max_norm: float32 [], replicated
Outputs:
- output 1: float32 [8, 512, 2048], P('stage')
- output 2: float32 [8, 2048, 512], P('stage')
- output 3: float32 [8, 512, 2048], P('stage')
- output 4: float32 [8, 2048, 512], P('stage')
- output 5: float32 [8, 512, 2048], P('stage')
- output 6: float32 [8, 2048, 512], P('stage')
- output 7: bfloat16 [8, 16, 2048, 512], P('stage', None, 'data')
All inputs are finite; a program needn't handle non-finite values.
Results may differ from a plain program's by a relative error of at most 0.012201.
Values are sent between devices in bfloat16 or wider.
A program may use at most 1 GiB of HBM per device.

v0:
```python
import functools

import jax
import jax.numpy as jnp
from jax import lax
from jax.experimental import pallas as pl
from jax.experimental.pallas import tpu as pltpu
from jax.sharding import PartitionSpec as P

BETA1 = 0.9
BETA2 = 0.95
ADAM_EPS = 1e-8
WEIGHT_DECAY = 0.1
NORM_EPS = 1e-6
ADAM_STEP = 8
SQRT_TWO_PI = 0.7978845608028654
GELU_CUBIC = 0.044715

MESH = pl.DeviceIdType.MESH
F32 = jnp.float32
BF16 = jnp.bfloat16


def tanh_part(pre_act):
    return jnp.tanh(SQRT_TWO_PI * (pre_act + GELU_CUBIC * pre_act * pre_act * pre_act))


def gelu_tanh(pre_act):
    return 0.5 * pre_act * (1.0 + tanh_part(pre_act))


def gelu_pair(pre_act):
    tanh_val = tanh_part(pre_act)
    act_value = 0.5 * pre_act * (1.0 + tanh_val)
    act_slope = 0.5 * (1.0 + tanh_val) + 0.5 * pre_act * (1.0 - tanh_val * tanh_val) * SQRT_TWO_PI * (1.0 + 3.0 * GELU_CUBIC * pre_act * pre_act)
    return act_value, act_slope


def mat(left, right):
    return jnp.dot(left, right, preferred_element_type=F32)


def mat_nt(left, right):
    return lax.dot_general(left, right, (((1,), (1,)), ((), ())), preferred_element_type=F32)


def adamw_update(master, first_mom, second_mom, grad_avg, clip_scale, learn_rate):
    scaled = clip_scale * grad_avg
    new_first = BETA1 * first_mom + (1.0 - BETA1) * scaled
    new_second = BETA2 * second_mom + (1.0 - BETA2) * scaled * scaled
    first_hat = new_first * (1.0 / (1.0 - BETA1 ** ADAM_STEP))
    second_hat = new_second * (1.0 / (1.0 - BETA2 ** ADAM_STEP))
    new_master = master - learn_rate * (first_hat / (jnp.sqrt(second_hat) + ADAM_EPS) + WEIGHT_DECAY * master)
    return new_master, new_first, new_second


class Cfg:
    def __init__(self, reps, stages, width, hidden, rows, micro):
        self.R, self.S, self.D, self.FF, self.T, self.M = reps, stages, width, hidden, rows, micro
        self.nblk = hidden // width
        self.hb = self.nblk // 2
        self.NB = 4
        self.BR = rows // self.NB
        self.CR = width // 16
        self.K = hidden // self.CR
        self.CG = width // 8
        self.KG = hidden // self.CG
        self.UR = rows // 4
        self.NU = micro * rows // self.UR
        self.LAG_MID = 3
        self.LAG_END = 16
        self.GLAG_MID = 2
        self.GLAG_END = 8


def mega(cfg, lr_ref, mn_ref, acts, mu, md, dy, gu, gd, m1u, m1d, m2u, m2d, nb,
         own, cvec, ys,
         rbuf, wbuf, xin, gin, gout, slope, mst, av, at, sq, cbuf,
         ld_sem, ldw_sem, ldg_sem, ldm_sem, g_recv, g_send, rs_recv, rs_send, c_recv, c_send, w_send,
         gb_recv, gb_send, x_recv, y_send):
    R, S, D, FF, T, M = cfg.R, cfg.S, cfg.D, cfg.FF, cfg.T, cfg.M
    CG, KG = cfg.CG, cfg.KG
    nblk, hb, NB, BR, CR, K, UR, NU = cfg.nblk, cfg.hb, cfg.NB, cfg.BR, cfg.CR, cfg.K, cfg.UR, cfg.NU
    r = lax.axis_index("data")
    s = lax.axis_index("stage")
    last = S - 1
    is_end = (r == 0) | (r == R - 1)
    is_mid = jnp.logical_not(is_end)
    low = r < R // 2

    UB, VB, UT, VT = 0, FF, 2 * FF, 3 * FF
    HT, DP = 0, FF

    def ru(c):
        return (c // hb) * FF + (c % hb) * D

    def rv(c):
        return ru(c) + FF // 2

    def ds(start, size):
        return pl.ds(pl.multiple_of(start, size), size)

    barrier = pltpu.get_barrier_semaphore()

    @pl.loop(0, R * S)
    def _(dev):
        pl.semaphore_signal(barrier, inc=1, device_id=(dev // S, dev % S), device_id_type=MESH)

    act_load = pltpu.make_async_copy(acts, av, ld_sem)
    act_load.start()
    w_loads = []
    for c in range(nblk):
        w_loads.append(pltpu.make_async_copy(mu.at[:, c * D:(c + 1) * D], own.at[ru(c):ru(c) + D, :], ldw_sem.at[c]))
    for c in range(nblk):
        w_loads.append(pltpu.make_async_copy(md.at[c * D:(c + 1) * D, :], own.at[rv(c):rv(c) + D, :], ldw_sem.at[nblk + c]))
    for load in w_loads:
        load.start()

    @pl.when(s == last)
    def _():
        for j in range(NB):
            pltpu.make_async_copy(dy.at[j * BR:(j + 1) * BR, :], gin.at[j * BR:(j + 1) * BR, :], g_recv.at[j]).start()

    g_loads = []
    for c in range(nblk):
        g_loads.append(pltpu.make_async_copy(gu.at[:, c * D:(c + 1) * D], own.at[ru(c):ru(c) + D, :], ldg_sem))
        g_loads.append(pltpu.make_async_copy(gd.at[c * D:(c + 1) * D, :], own.at[rv(c):rv(c) + D, :], ldg_sem))

    act_load.wait()
    for c in range(nblk):
        w_loads[c].wait()
        xin[UB + c * D:UB + (c + 1) * D, :] = own[ru(c):ru(c) + D, :].astype(BF16)

    late = s >= S // 2

    def slope_part(j):
        for c in range(nblk):
            pre = mat(av[ds(j * BR, BR), :], xin[UB + c * D:UB + (c + 1) * D, :])
            _, act_slope = gelu_pair(pre)
            slope[ds(c * T + j * BR, BR), :] = act_slope

    @pl.loop(0, NB)
    def _(j):
        slope_part(j)

    for c in range(nblk):
        w_loads[nblk + c].wait()
        xin[VB + c * D:VB + (c + 1) * D, :] = own[rv(c):rv(c) + D, :].astype(BF16)
    for load in g_loads:
        load.start()

    def hidden_part(j):
        @pl.loop(0, nblk)
        def _(c):
            pre = mat(av[ds(j * BR, BR), :], xin[ds(UB + c * D, D), :])
            wbuf[ds(HT + c * D, D), ds(j * BR, BR)] = gelu_tanh(pre).T.astype(BF16)

    def transpose_acts():
        at[...] = av[...].astype(F32).T.astype(BF16)

    @pl.when(s < last)
    def _():
        @pl.loop(0, nblk)
        def _(c):
            xin[ds(UT + c * D, D), :] = xin[ds(UB + c * D, D), :].T
            xin[ds(VT + c * D, D), :] = xin[ds(VB + c * D, D), :].T

    @pl.when(jnp.logical_not(late))
    def _():
        @pl.loop(0, NB)
        def _(j):
            hidden_part(j)

        transpose_acts()

    with jax.named_scope("barrier_wait"):
        pl.semaphore_wait(barrier, R * S)

    def g_copy(j):
        rows = ds(j * BR, BR)
        return pltpu.make_async_remote_copy(gout.at[rows, :], gin.at[rows, :], g_send.at[j], g_recv.at[j],
                                            device_id={"stage": s - 1}, device_id_type=MESH)

    def chain_step(j, down_of, up_of):
        rows = ds(j * BR, BR)
        g = gin[rows, :]
        total = None
        for c in range(nblk):
            part = ds(c * T + j * BR, BR)
            d_pre = (down_of(g, c) * slope[part, :]).astype(BF16)
            wbuf[ds(DP + c * T + j * BR, BR), :] = d_pre
            if up_of is not None:
                piece = up_of(d_pre, c)
                total = piece if total is None else total + piece
        if up_of is not None:
            gout[rows, :] = (g.astype(F32) + total).astype(BF16)
            g_copy(j).start()

    def chain_wait(j):
        rows = ds(j * BR, BR)
        with jax.named_scope("chain_wait"):
            pltpu.make_async_copy(gin.at[rows, :], gin.at[rows, :], g_recv.at[j]).wait()

    def down_t(g, c):
        return mat(g, xin[VT + c * D:VT + (c + 1) * D, :])

    def up_t(d, c):
        return mat(d, xin[UT + c * D:UT + (c + 1) * D, :])

    @pl.when(s == last)
    def _():
        @pl.loop(0, NB)
        def _(j):
            chain_wait(j)
            chain_step(j, lambda g, c: mat_nt(g, xin[VB + c * D:VB + (c + 1) * D, :]),
                       lambda d, c: mat_nt(d, xin[UB + c * D:UB + (c + 1) * D, :]))

    @pl.when((s > 0) & (s < last))
    def _():
        @pl.loop(0, NB)
        def _(j):
            chain_wait(j)
            chain_step(j, down_t, up_t)

    @pl.when(s == 0)
    def _():
        @pl.loop(0, NB)
        def _(j):
            chain_wait(j)
            chain_step(j, down_t, None)

    @pl.when(late)
    def _():
        @pl.loop(0, NB)
        def _(j):
            hidden_part(j)

        transpose_acts()

    pltpu.make_async_copy(own, own, ldg_sem).wait()

    half_d = D // 2

    def add_weight_grads(j):
        @pl.when(j < hb)
        def _():
            for half in (0, 1):
                for m in (0, 1):
                    rows = ds(half * FF + j * D + m * half_d, half_d)
                    own[rows, :] += mat(at[m * half_d:(m + 1) * half_d, :], wbuf[ds(DP + (half * hb + j) * T, T), :])

        @pl.when(j >= hb)
        def _():
            for half in (0, 1):
                for m in (0, 1):
                    rows = ds(half * FF + j * D + m * half_d, half_d)
                    own[rows, :] += mat(wbuf[ds(HT + (half * hb + j - hb) * D + m * half_d, half_d), :], gin[...])

    def state_loads(half):
        spare = (1 - half) * FF
        out = []
        for b in range(hb):
            cols = slice((half * hb + b) * D, (half * hb + b + 1) * D)
            up, down = b * D, FF // 2 + b * D
            out.append(pltpu.make_async_copy(mu.at[:, cols], mst.at[up:up + D, :], ldm_sem.at[0]))
            out.append(pltpu.make_async_copy(md.at[cols, :], mst.at[down:down + D, :], ldm_sem.at[0]))
            out.append(pltpu.make_async_copy(m1u.at[:, cols], slope.at[up:up + D, :], ldm_sem.at[1]))
            out.append(pltpu.make_async_copy(m1d.at[cols, :], slope.at[down:down + D, :], ldm_sem.at[1]))
            out.append(pltpu.make_async_copy(m2u.at[:, cols], rbuf.at[spare + up:spare + up + D, :], ldm_sem.at[2]))
            out.append(pltpu.make_async_copy(m2d.at[cols, :], rbuf.at[spare + down:spare + down + D, :], ldm_sem.at[2]))
        return out

    def half_rows(half, k):
        return ds(half * FF + k * CR, CR)

    def await_f32(sem, half, k):
        rows = half_rows(half, k)
        pltpu.make_async_copy(own.at[rows, :], own.at[rows, :], sem.at[half, k]).wait()

    def rs_copy(src, half, k):
        rows = half_rows(half, k)
        return pltpu.make_async_remote_copy(src.at[rows, :], rbuf.at[rows, :], rs_send.at[half], rs_recv.at[half, k],
                                            device_id={"data": r + 2 * half - 1}, device_id_type=MESH)

    def half_sent(ref, sem, half):
        rows = ds(half * FF, FF)
        pltpu.make_async_copy(ref.at[rows, :], ref.at[rows, :], sem.at[half]).wait()

    rs_near = jnp.where(low, 1, 0)
    rs_far = 1 - rs_near
    lag = jnp.where(is_end, cfg.LAG_END, cfg.LAG_MID)
    sq[...] = jnp.zeros_like(sq)

    per_block = D // CR

    @pl.loop(0, K + cfg.LAG_END)
    def _(i):
        @pl.when((i % per_block == 0) & (i < K))
        def _():
            with jax.named_scope("weight_grads"):
                add_weight_grads(i // per_block)

        for half, where in ((0, r == 0), (1, r == R - 1)):
            @pl.when(where & (i == K // 2))
            def _():
                for load in state_loads(half):
                    load.start()

        @pl.when((i < K) & is_end)
        def _():
            rs_copy(own, rs_near, i).start()

        @pl.when((i < K) & is_mid)
        def _():
            await_f32(rs_recv, rs_near, i)
            rows = half_rows(rs_near, i)
            rbuf[rows, :] += own[rows, :]
            rs_copy(rbuf, rs_near, i).start()

        k = i - lag

        @pl.when((k >= 0) & (k < K) & is_mid)
        def _():
            with jax.named_scope("rs_far_wait"):
                await_f32(rs_recv, rs_far, k)
            rows = half_rows(rs_far, k)
            rbuf[rows, :] += own[rows, :]
            rs_copy(rbuf, rs_far, k).start()

        @pl.when((k >= 0) & (k < K) & is_end)
        def _():
            with jax.named_scope("rs_end_wait"):
                await_f32(rs_recv, rs_far, k)
            rows = half_rows(rs_far, k)
            mean = (own[rows, :] + rbuf[rows, :]) * (1.0 / R)
            own[rows, :] = mean
            sq[...] += jnp.sum((mean * mean).reshape(CR // 8, 8, D), axis=0)

    mine = jnp.where(r == 0, s, S + s)
    me = r * S + s

    def c_copy(dev):
        return pltpu.make_async_remote_copy(cbuf.at[mine], cbuf.at[mine], c_send, c_recv.at[mine],
                                            device_id=(dev // S, dev % S), device_id_type=MESH)

    @pl.when(is_end)
    def _():
        part = sq[:, 0:128]
        for q in range(1, D // 128):
            part = part + sq[:, q * 128:(q + 1) * 128]
        cbuf[mine] = part

        half_sent(own, rs_send, rs_near)

        @pl.loop(0, R * S)
        def _(dev):
            @pl.when(dev != me)
            def _():
                c_copy(dev).start()

    @pl.when(s == 0)
    def _():
        def load(k, start, size):
            pltpu.make_async_copy(nb.at[ds(start, size), :], xin.at[ds(start, size), :], x_recv.at[k]).start()

        @pl.loop(0, NU - 1)
        def _(u):
            load(u, u * UR, UR)

        for v in range(2):
            load(NU - 1 + v, (NU - 1) * UR + v * (UR // 2), UR // 2)

    with jax.named_scope("clip_wait"):
        @pl.loop(0, 2 * S)
        def _(slot):
            @pl.when(is_mid | (slot != mine))
            def _():
                pltpu.make_async_copy(cbuf.at[slot], cbuf.at[slot], c_recv.at[slot]).wait()

    total_sq = cbuf[0]
    for slot in range(1, 2 * S):
        total_sq = total_sq + cbuf[slot]
    total_sq = jnp.sum(jnp.sum(total_sq, axis=0, keepdims=True), axis=1, keepdims=True)
    grad_norm = jnp.sqrt(jnp.broadcast_to(total_sq, (8, 128)))
    cvec[...] = jnp.minimum(1.0, mn_ref[0] / (grad_norm + NORM_EPS))

    @pl.when(is_end)
    def _():
        for n in range(3):
            pltpu.make_async_copy(mst, mst, ldm_sem.at[n]).wait()

    ag_near = 1 - rs_near
    ag_far = rs_near

    def gb_rows(half, k):
        return ds(half * FF + k * CG, CG)

    def w_copy(half, k):
        rows = gb_rows(half, k)
        return pltpu.make_async_remote_copy(wbuf.at[rows, :], wbuf.at[rows, :], w_send.at[half], rs_recv.at[half, k],
                                            device_id={"data": r + 1 - 2 * half}, device_id_type=MESH)

    def await_w(half, k):
        rows = gb_rows(half, k)
        pltpu.make_async_copy(wbuf.at[rows, :], wbuf.at[rows, :], rs_recv.at[half, k]).wait()

    @pl.loop(0, KG + cfg.GLAG_MID)
    def _(i):
        @pl.when((i < KG) & is_end)
        def _():
            rows = gb_rows(ag_near, i)
            local = ds(i * CG, CG)
            clip = cvec[0:1, 0:1]
            new_master, _, _ = adamw_update(mst[local, :], slope[local, :], rbuf[gb_rows(rs_near, i), :], own[rows, :], clip, lr_ref[0])
            wbuf[rows, :] = new_master.astype(BF16)
            w_copy(ag_near, i).start()

        @pl.when((i < KG) & is_mid)
        def _():
            with jax.named_scope("w_near_wait"):
                await_w(ag_near, i)
            w_copy(ag_near, i).start()

        k = i - cfg.GLAG_MID

        @pl.when((k >= 0) & is_mid)
        def _():
            await_w(ag_far, k)
            w_copy(ag_far, k).start()

    def await_gb(half, k):
        rows = gb_rows(half, k)
        pltpu.make_async_copy(own.at[rows, :], own.at[rows, :], gb_recv.at[half, k]).wait()

    def gb_copy(half, k):
        rows = gb_rows(half, k)
        return pltpu.make_async_remote_copy(own.at[rows, :], own.at[rows, :], gb_send.at[half], gb_recv.at[half, k],
                                            device_id={"data": r + 1 - 2 * half}, device_id_type=MESH)

    g_lag = jnp.where(is_end, cfg.GLAG_END, cfg.GLAG_MID)

    def z_step(i):
        @pl.when(i < KG)
        def _():
            @pl.when(is_mid)
            def _():
                await_gb(ag_near, i)
                gb_copy(ag_near, i).start()

        k = i - g_lag

        @pl.when((k >= 0) & (k < KG))
        def _():
            await_gb(ag_far, k)

            @pl.when(is_mid)
            def _():
                gb_copy(ag_far, k).start()

    @pl.when(is_end)
    def _():
        @pl.loop(0, KG)
        def _(k):
            gb_copy(ag_near, k).start()

        @pl.loop(0, KG)
        def _(k):
            with jax.named_scope("w_end_wait"):
                await_w(ag_far, k)

    def y_copy(k, rows):
        return pltpu.make_async_remote_copy(ys.at[rows, :], xin.at[rows, :], y_send, x_recv.at[k],
                                            device_id={"stage": s + 1}, device_id_type=MESH)

    def unit(k, start, size):
        rows = ds(start, size)

        with jax.named_scope("x_wait"):
            pltpu.make_async_copy(xin.at[rows, :], xin.at[rows, :], x_recv.at[k]).wait()
        x = xin[rows, :]
        total = None
        for c in range(nblk):
            hid = gelu_tanh(mat(x, wbuf[ru(c):ru(c) + D, :])).astype(BF16)
            piece = mat(hid, wbuf[rv(c):rv(c) + D, :])
            total = piece if total is None else total + piece
        ys[rows, :] = (x.astype(F32) + total).astype(BF16)

        @pl.when(s < last)
        def _():
            y_copy(k, rows).start()

    z_total = KG + cfg.GLAG_END
    z_pre = s - 1

    with jax.named_scope("z_pre"):
        @pl.loop(0, z_pre)
        def _(i):
            z_step(i)

    @pl.loop(0, NU - 1)
    def _(u):
        unit(u, u * UR, UR)

        @pl.when((u % 2 == 1) & (u // 2 + z_pre >= 0))
        def _():
            with jax.named_scope("z_step"):
                z_step(u // 2 + z_pre)

    @pl.loop(0, 2)
    def _(v):
        unit(NU - 1 + v, (NU - 1) * UR + v * (UR // 2), UR // 2)

    with jax.named_scope("z_tail"):
        @pl.loop((NU - 1) // 2 + z_pre, z_total)
        def _(i):
            z_step(i)

    @pl.when(s < last)
    def _():
        pltpu.make_async_copy(ys, ys, y_send).wait()

    @pl.when(s > 0)
    def _():
        @pl.loop(0, NB)
        def _(j):
            g_copy(j).wait_send()

    @pl.when(is_end)
    def _():
        pltpu.make_async_copy(cbuf.at[0:R * S - 1], cbuf.at[0:R * S - 1], c_send).wait()

    half_sent(wbuf, w_send, ag_near)
    half_sent(own, gb_send, ag_near)

    @pl.when(is_mid)
    def _():
        half_sent(rbuf, rs_send, rs_near)
        half_sent(rbuf, rs_send, rs_far)
        half_sent(wbuf, w_send, ag_far)
        half_sent(own, gb_send, ag_far)


def mega_call(cfg, lr, mn, acts, mu, md, dy, gu, gd, m1u, m1d, m2u, m2d, nb):
    D, FF, T, M = cfg.D, cfg.FF, cfg.T, cfg.M
    any_spec = pl.BlockSpec(memory_space=pl.ANY)
    smem = pl.BlockSpec(memory_space=pltpu.SMEM)
    vmem_spec = pl.BlockSpec(memory_space=pltpu.VMEM)
    dma = pltpu.SemaphoreType.DMA
    return pl.pallas_call(
        functools.partial(mega, cfg),
        out_shape=(
            pltpu.VMEM((2 * FF, D), F32),
            pltpu.VMEM((8, 128), F32),
            pltpu.VMEM((M * T, D), BF16),
        ),
        in_specs=[smem, smem] + [pl.BlockSpec(memory_space=pltpu.HBM)] * 11,
        out_specs=(vmem_spec,) * 3,
        scratch_shapes=[
            pltpu.VMEM((2 * FF, D), F32),
            pltpu.VMEM((2 * FF, D), BF16),
            pltpu.VMEM((M * T, D), BF16),
            pltpu.VMEM((T, D), BF16),
            pltpu.VMEM((T, D), BF16),
            pltpu.VMEM((max(cfg.nblk * T, FF), D), F32),
            pltpu.VMEM((FF, D), F32),
            pltpu.VMEM((T, D), BF16),
            pltpu.VMEM((D, T), BF16),
            pltpu.VMEM((8, D), F32),
            pltpu.VMEM((cfg.R * cfg.S, 8, 128), F32),
            dma,
            dma((2 * cfg.nblk,)),
            dma,
            dma((3,)),
            dma((cfg.NB,)),
            dma((cfg.NB,)),
            dma((2, cfg.K)),
            dma((2,)),
            dma((2 * cfg.S,)),
            dma,
            dma((2,)),
            dma((2, cfg.KG)),
            dma((2,)),
            dma((cfg.NU + 1,)),
            dma,
        ],
        compiler_params=pltpu.CompilerParams(
            collective_id=0, has_side_effects=True, vmem_limit_bytes=32 * 1024 * 1024),
        cost_estimate=pl.CostEstimate(flops=200_000_000_000, bytes_accessed=100_000_000, transcendentals=0),
        name="pipeline_step",
    )(lr, mn, *[pltpu.with_memory_space_constraint(x, pltpu.HBM) for x in (acts, mu, md, dy, gu, gd, m1u, m1d, m2u, m2d, nb)])


def finish(steps, lr_ref, clip_ref, grads, rows_in, h0, h1, h2, s0, s1, s2,
           new_u, new_d, new_m1u, new_m1d, new_m2u, new_m2d, rows_out,
           v0, v1, v2, ou, od, om1u, om1d, om2u, om2d, in_sem, out_sem, row_sem):
    mu, md, m1u, m1d, m2u, m2d = h0, v0, h1, v1, h2, v2
    outs = ((ou, new_u), (om1u, new_m1u), (om2u, new_m2u), (od, new_d), (om1d, new_m1d), (om2d, new_m2d))
    slots = ou.shape[0]
    width, hidden = mu.shape
    blocks = hidden // width

    def part(x, i):
        size = x.shape[0] // steps
        return pl.ds(pl.multiple_of(i * size, size), size)

    def row_write(i):
        return pltpu.make_async_copy(rows_in.at[part(rows_in, i), :], rows_out.at[part(rows_in, i), :], row_sem)

    def write(n, i):
        src, dst = outs[n]
        return pltpu.make_async_copy(src.at[i % slots], dst.at[part(dst, i), :], out_sem.at[n // 3, i % slots])

    def state_reads(i):
        return [pltpu.make_async_copy(src.at[part(src, i), :], dst.at[part(src, i), :], in_sem.at[i])
                for src, dst in ((s0, v0), (s1, v1), (s2, v2))]

    @pl.loop(0, steps)
    def _(i):
        for copy in state_reads(i):
            copy.start()

    clip = clip_ref[0:1, 0:1]

    @pl.loop(0, steps)
    def _(i):
        @pl.when(i >= slots)
        def _():
            for n in range(3):
                write(n, i - slots).wait()

        p = part(mu, i)
        for c in range(blocks):
            cols = slice(c * width, (c + 1) * width)
            first = (c // (blocks // 2)) * hidden + (c % (blocks // 2)) * width
            g = grads[pl.ds(pl.multiple_of(first + i * (width // steps), width // steps), width // steps), :]
            new = adamw_update(mu[p, cols], m1u[p, cols], m2u[p, cols], g, clip, lr_ref[0])
            for (dst, _), val in zip(outs[0:3], new):
                dst[i % slots, :, cols] = val
        for n in range(3):
            write(n, i).start()
        row_write(i).start()

    @pl.loop(0, steps)
    def _(i):
        @pl.when(i >= slots)
        def _():
            for n in range(3, 6):
                write(n, i - slots).wait()

        for copy in state_reads(i):
            copy.wait()
        p = part(md, i)
        size = hidden // steps
        low = i * size
        first = jnp.where(low < hidden // 2, hidden // 2 + low, hidden + low)
        g = grads[pl.ds(pl.multiple_of(first, size), size), :]
        for (dst, _), val in zip(outs[3:6], adamw_update(md[p, :], m1d[p, :], m2d[p, :], g, clip, lr_ref[0])):
            dst[i % slots] = val
        for n in range(3, 6):
            write(n, i).start()

    @pl.loop(steps - slots, steps)
    def _(i):
        for n in range(len(outs)):
            write(n, i).wait()

    pltpu.make_async_copy(rows_in, rows_out, row_sem).wait()


def finish_call(lr, clip, grads, mu, md, m1u, m1d, m2u, m2d, rows_in, steps):
    states = (mu, md, m1u, m1d, m2u, m2d)
    held, streamed = (mu, m1u, m2u), (md, m1d, m2d)
    outs = states + (rows_in,)
    any_spec = pl.BlockSpec(memory_space=pl.ANY)
    vmem_spec = pl.BlockSpec(memory_space=pltpu.VMEM)
    slots = 3

    def ring(x, n):
        return pltpu.VMEM((n, x.shape[0] // steps, x.shape[1]), x.dtype)

    dma = pltpu.SemaphoreType.DMA
    return pl.pallas_call(
        functools.partial(finish, steps),
        out_shape=tuple(jax.ShapeDtypeStruct(x.shape, x.dtype) for x in outs),
        in_specs=[pl.BlockSpec(memory_space=pltpu.SMEM), vmem_spec, vmem_spec, vmem_spec] + [vmem_spec] * 3 + [pl.BlockSpec(memory_space=pltpu.HBM)] * 3,
        out_specs=(any_spec,) * len(outs),
        scratch_shapes=[pltpu.VMEM(x.shape, F32) for x in streamed]
        + [ring(x, slots) for x in states] + [dma((steps,)), dma((2, slots)), dma],
        compiler_params=pltpu.CompilerParams(vmem_limit_bytes=20 * 1024 * 1024),
        cost_estimate=pl.CostEstimate(flops=100_000_000, bytes_accessed=75_000_000, transcendentals=0),
        name="finish",
    )(lr, clip, grads, rows_in, *[pltpu.with_memory_space_constraint(x, pltpu.VMEM) for x in held],
      *[pltpu.with_memory_space_constraint(x, pltpu.HBM) for x in streamed])


def solution(mesh):
    n_stages = mesh.shape['stage']
    n_reps = mesh.shape['data']

    def local_step(master_up, master_down, mom1_up, mom1_down, mom2_up, mom2_down, grad_up, grad_down, stage_acts, loss_grad, next_batch, learn_rate, max_norm):
        n_micro, rows, width = next_batch.shape
        hidden = master_up.shape[2]
        cfg = Cfg(n_reps, n_stages, width, hidden, rows, n_micro)
        grads, clip, outs = mega_call(
            cfg, learn_rate.reshape(1), max_norm.reshape(1), stage_acts[0], master_up[0], master_down[0], loss_grad,
            grad_up[0, 0], grad_down[0, 0], mom1_up[0], mom1_down[0], mom2_up[0], mom2_down[0],
            next_batch.reshape(n_micro * rows, width))
        new_up, new_down, new_m1_up, new_m1_down, new_m2_up, new_m2_down, outs = finish_call(
            learn_rate.reshape(1), clip, grads, master_up[0], master_down[0], mom1_up[0], mom1_down[0],
            mom2_up[0], mom2_down[0], outs, 16)
        stage_outs = outs.reshape(1, n_micro, rows, width)
        return (new_up[None], new_down[None], new_m1_up[None], new_m1_down[None], new_m2_up[None], new_m2_down[None], stage_outs)

    w_spec = P('stage', None, None)
    g_spec = P('data', 'stage', None, None)
    in_specs = (w_spec, w_spec, w_spec, w_spec, w_spec, w_spec, g_spec, g_spec, P('stage', 'data', None), P('data', None), P(None, 'data', None), P(), P())
    out_specs = (w_spec, w_spec, w_spec, w_spec, w_spec, w_spec, P('stage', None, 'data', None))
    return jax.shard_map(local_step, mesh=mesh, in_specs=in_specs, out_specs=out_specs, check_vma=False)
```

profile of v0, /device:TPU:7, one launch (start us, length us, event | category | flops | bytes accessed | tf_op | source)
XLA Modules:
  0.0 330.3 jit_solution(9468319892329875198)
XLA Ops:
  1.9 0.0 copy-start
  1.9 0.0 copy-start.1
  1.9 0.0 copy-start.2
  2.0 311.7 %pipeline_step.1 = (f32[4096,512]{1,0:T(8,128)S(1)}, f32[8,128]{1,0:T(8,128)S(1)}, bf16[8192,512]{1,0:T(8,128)(2,1)S(1)}) custom-call(f32[1]{0:T(128)} %bitcast.19.lr_ref, f32[1]{0:T(128)} %bitcast.21.mn_ref, bf16[512,512]{1,0:T(8,128)(2,1)} %bitcast.44, f32[512,2048]{1,0:T(8,128)} %bitcast.22, f32[2048,512]{1,0:T(8,128)} %bitcast.28, bf16[512,512]{1,0:T(8,128)(2,1)} %dy.1, ...), custom_call_target="tpu_custom_call" | custom-call | flops 199999995904 | bytes 100000000 | tf_op jit(solution)/shard_map/pipeline_step/pallas_call | solution.py:549
  313.6 0.0 copy-done
  313.7 0.0 copy-done.1
  313.7 0.0 copy-done.2
  313.7 16.6 %finish.1 = (f32[512,2048]{1,0:T(8,128)}, f32[2048,512]{1,0:T(8,128)}, f32[512,2048]{1,0:T(8,128)}, f32[2048,512]{1,0:T(8,128)}, f32[512,2048]{1,0:T(8,128)}, /*...) custom-call(f32[1]{0:T(128)} %bitcast.20.lr_ref, f32[8,128]{1,0:T(8,128)S(1)} %get-tuple-element.17.clip_ref, ...), custom_call_target="tpu_custom_call" | custom-call | flops 100000000 | bytes 75000000 | tf_op jit(solution)/shard_map/finish/pallas_call | solution.py:682
Async XLA Ops:
  1.9 311.7 %copy-start = (f32[1,512,2048]{2,1,0:T(8,128)S(1)}, f32[1,512,2048]{2,1,0:T(8,128)}, u32[]{:S(2)}) copy-start(f32[1,512,2048]{2,1,0:T(8,128)} %param.13) | copy-start | bytes 12582916
  1.9 311.7 %copy-start.1 = (f32[1,512,2048]{2,1,0:T(8,128)S(1)}, f32[1,512,2048]{2,1,0:T(8,128)}, u32[]{:S(2)}) copy-start(f32[1,512,2048]{2,1,0:T(8,128)} %param.15) | copy-start | bytes 12582916
  1.9 311.7 %copy-start.2 = (f32[1,512,2048]{2,1,0:T(8,128)S(1)}, f32[1,512,2048]{2,1,0:T(8,128)}, u32[]{:S(2)}) copy-start(f32[1,512,2048]{2,1,0:T(8,128)} %param.17) | copy-start | bytes 12582916
where the time goes:
time: 330 us
  Pallas kernels  328 us (99%)
    pallas_call x1, Pallas kernels, mega_call(): pl.pallas_call(functools.partial(mega, cfg), out_shape=(pltpu.VMEM((2 * F...  312 us
    pallas_call x1, Pallas kernels, finish_call(): pl.pallas_call(functools.partial(finish, steps), out_shape=tuple((jax.Sha...  16.6 us

commit v1 on v0

--- a/solution.py
+++ b/solution.py
@@ -77,7 +77,7 @@
          own, cvec, ys,
          rbuf, wbuf, xin, gin, gout, slope, mst, av, at, sq, cbuf,
          ld_sem, ldw_sem, ldg_sem, ldm_sem, g_recv, g_send, rs_recv, rs_send, c_recv, c_send, w_send,
-         gb_recv, gb_send, x_recv, y_send):
+         gb_send, x_recv, y_send):
     R, S, D, FF, T, M = cfg.R, cfg.S, cfg.D, cfg.FF, cfg.T, cfg.M
     CG, KG = cfg.CG, cfg.KG
     nblk, hb, NB, BR, CR, K, UR, NU = cfg.nblk, cfg.hb, cfg.NB, cfg.BR, cfg.CR, cfg.K, cfg.UR, cfg.NU
@@ -139,9 +139,13 @@
             _, act_slope = gelu_pair(pre)
             slope[ds(c * T + j * BR, BR), :] = act_slope
 
-    @pl.loop(0, NB)
-    def _(j):
-        slope_part(j)
+    slope_part(0)
+
+    @pl.when(s < last - 1)
+    def _():
+        @pl.loop(1, NB)
+        def _(j):
+            slope_part(j)
 
     for c in range(nblk):
         w_loads[nblk + c].wait()
@@ -215,12 +219,20 @@
             chain_step(j, lambda g, c: mat_nt(g, xin[VB + c * D:VB + (c + 1) * D, :]),
                        lambda d, c: mat_nt(d, xin[UB + c * D:UB + (c + 1) * D, :]))
 
+            @pl.when(j + 1 < NB)
+            def _():
+                slope_part(j + 1)
+
     @pl.when((s > 0) & (s < last))
     def _():
         @pl.loop(0, NB)
         def _(j):
             chain_wait(j)
             chain_step(j, down_t, up_t)
+
+            @pl.when((s == last - 1) & (j + 1 < NB))
+            def _():
+                slope_part(j + 1)
 
     @pl.when(s == 0)
     def _():
@@ -430,11 +442,11 @@
 
     def await_gb(half, k):
         rows = gb_rows(half, k)
-        pltpu.make_async_copy(own.at[rows, :], own.at[rows, :], gb_recv.at[half, k]).wait()
+        pltpu.make_async_copy(own.at[rows, :], own.at[rows, :], rs_recv.at[half, KG + k]).wait()
 
     def gb_copy(half, k):
         rows = gb_rows(half, k)
-        return pltpu.make_async_remote_copy(own.at[rows, :], own.at[rows, :], gb_send.at[half], gb_recv.at[half, k],
+        return pltpu.make_async_remote_copy(own.at[rows, :], own.at[rows, :], gb_send.at[half], rs_recv.at[half, KG + k],
                                             device_id={"data": r + 1 - 2 * half}, device_id_type=MESH)
 
     g_lag = jnp.where(is_end, cfg.GLAG_END, cfg.GLAG_MID)
@@ -578,7 +590,6 @@
             dma((2 * cfg.S,)),
             dma,
             dma((2,)),
-            dma((2, cfg.KG)),
             dma((2,)),
             dma((cfg.NU + 1,)),
             dma,

time: 330 us -> 330 us (level)
  no operation moved by 1% of the time
where the time goes in v1:
time: 330 us
  Pallas kernels  328 us (99%)
    pallas_call x1, Pallas kernels, mega_call(): pl.pallas_call(functools.partial(mega, cfg), out_shape=(pltpu.VMEM((2 * F...  311 us
    pallas_call x1, Pallas kernels, finish_call(): pl.pallas_call(functools.partial(finish, steps), out_shape=tuple((jax.Sha...  16.6 us

profile of v1, /device:TPU:7, one launch (start us, length us, event | category | flops | bytes accessed | tf_op | source)
XLA Modules:
  0.0 329.7 jit_solution(6461266722439404494)
XLA Ops:
  1.9 0.0 copy-start
  1.9 0.0 copy-start.1
  1.9 0.0 copy-start.2
  2.0 311.1 %pipeline_step.1 = (f32[4096,512]{1,0:T(8,128)S(1)}, f32[8,128]{1,0:T(8,128)S(1)}, bf16[8192,512]{1,0:T(8,128)(2,1)S(1)}) custom-call(f32[1]{0:T(128)} %bitcast.19.lr_ref, f32[1]{0:T(128)} %bitcast.21.mn_ref, bf16[512,512]{1,0:T(8,128)(2,1)} %bitcast.44, f32[512,2048]{1,0:T(8,128)} %bitcast.22, f32[2048,512]{1,0:T(8,128)} %bitcast.28, bf16[512,512]{1,0:T(8,128)(2,1)} %dy.1, ...), custom_call_target="tpu_custom_call" | custom-call | flops 199999995904 | bytes 100000000 | tf_op jit(solution)/shard_map/pipeline_step/pallas_call | solution.py:561
  313.1 0.0 copy-done
  313.1 0.0 copy-done.1
  313.1 0.0 copy-done.2
  313.1 16.6 %finish.1 = (f32[512,2048]{1,0:T(8,128)}, f32[2048,512]{1,0:T(8,128)}, f32[512,2048]{1,0:T(8,128)}, f32[2048,512]{1,0:T(8,128)}, f32[512,2048]{1,0:T(8,128)}, /*...) custom-call(f32[1]{0:T(128)} %bitcast.20.lr_ref, f32[8,128]{1,0:T(8,128)S(1)} %get-tuple-element.17.clip_ref, ...), custom_call_target="tpu_custom_call" | custom-call | flops 100000000 | bytes 75000000 | tf_op jit(solution)/shard_map/finish/pallas_call | solution.py:693
Async XLA Ops:
  1.9 311.2 %copy-start = (f32[1,512,2048]{2,1,0:T(8,128)S(1)}, f32[1,512,2048]{2,1,0:T(8,128)}, u32[]{:S(2)}) copy-start(f32[1,512,2048]{2,1,0:T(8,128)} %param.13) | copy-start | bytes 12582916
  1.9 311.2 %copy-start.1 = (f32[1,512,2048]{2,1,0:T(8,128)S(1)}, f32[1,512,2048]{2,1,0:T(8,128)}, u32[]{:S(2)}) copy-start(f32[1,512,2048]{2,1,0:T(8,128)} %param.15) | copy-start | bytes 12582916
  1.9 311.2 %copy-start.2 = (f32[1,512,2048]{2,1,0:T(8,128)S(1)}, f32[1,512,2048]{2,1,0:T(8,128)}, u32[]{:S(2)}) copy-start(f32[1,512,2048]{2,1,0:T(8,128)} %param.17) | copy-start | bytes 12582916
